TPU v7x, 32 devices: a whole 2x2x4 slice. The times are simulated.
32 devices in a mesh: dp: 16 (over z, y, x), tensor: 2 (over core).
Axes of the slice: x: 2, y: 2, z: 4, core: 2. Of those that a mesh axis runs over, the one named last changes fastest.
Arguments:
- encoded: bfloat16 [8192, 1152], P('dp', 'tensor'), may hold values from -9 to 9
- counts: int32 [128], P('dp'), may hold values from 16 to 64
- win_ids: int32 [128, 64], P('dp'), may hold values from 0 to 31, never falling along the last dimension, each value on 1 to 8 neighbouring positions
- dest_seq: int32 [128], P('dp'), may hold values from 0 to 15, as said below
- dest_slot: int32 [128], P('dp'), may hold values from 0 to 7, as said below
- w_first: bfloat16 [1152, 4608], P(None, 'tensor'), may hold values from -0.3125 to 0.3125
- b_first: float32 [4608], P('tensor'), may hold values from -3 to 3
- w_second: bfloat16 [4608, 2304], P('tensor'), may hold values from -0.1875 to 0.1875
- b_second: float32 [2304], P('tensor'), may hold values from -3 to 3
Outputs:
- projected: bfloat16 [4096, 2304], P('dp', 'tensor')
Inputs may be any that keep to these rules, and one draw needn't show every extreme that they name: `dest_seq`: every sequence receives exactly 8 samples, no two of them from the same index of dp. `dest_slot`: the samples that one sequence receives have distinct block offsets.
All inputs are finite; a program needn't handle non-finite values.
Results may differ from a plain program's by a relative error of at most 0.009.
Values may be sent and summed in bfloat16 or wider, within the bound.
A program may use at most 128 MiB of HBM per device.

v0:
```python
import functools
import math

import jax
import jax.numpy as jnp
from jax import lax
from jax.experimental import pallas as pl
from jax.experimental.pallas import tpu as pltpu
from jax.sharding import PartitionSpec as P

BLOCK = 32
LANES = 128
MESH = pl.DeviceIdType.MESH
UNROLL_MAX = 16


def loop(count, body):
    if count <= UNROLL_MAX:
        for i in range(count):
            body(i)
    else:

        @pl.loop(0, count)
        def _(i):
            body(i)


def col_chunks(width, step):
    return [(lo, min(step, width - lo)) for lo in range(0, width, step)]


def gelu(x):
    c0 = math.sqrt(2.0 / math.pi)
    half = 0.5 * x
    return half + half * jnp.tanh(x * (c0 + (c0 * 0.044715) * (x * x)))


def kernel(
    dims,
    seq_s, slot_s, cnt_s, win_v, b1_v, b2_v, enc_h, w1_h, w2_h,
    out_v,
    enc, w1, w2, pooled, outgo, arr, sib, route_src, routes, xbuf, hidden, part_out, part_in,
    load_sem, w1_sem, w2_sem, send_sem, recv_sem, rsend_sem, rrecv_sem, fsend_sem, frecv_sem,
    psend_sem, precv_sem,
):
    groups, samples, cap, feat = dims
    full = feat // LANES
    rem = feat - full * LANES
    me = lax.axis_index("dp")
    core = lax.axis_index("tensor")
    other = 1 - core

    barrier = pltpu.get_barrier_semaphore()
    pl.semaphore_signal(barrier, 1, device_id={"tensor": other}, device_id_type=MESH)

    def greet(i):
        peer = lax.rem(me + 1 + i, groups)
        pl.semaphore_signal(barrier, 1, device_id={"dp": peer}, device_id_type=MESH)

    loop(groups - 1, greet)

    pairs = enc.shape[0]
    enc_copies = [
        pltpu.make_async_copy(enc_h.at[:, p * LANES : (p + 1) * LANES], enc.at[p], load_sem.at[p])
        for p in range(pairs)
    ]
    for copy in enc_copies:
        copy.start()

    wide = full * LANES
    mine = pl.multiple_of(core * feat, 64)
    theirs = pl.multiple_of(other * feat, 64)
    spans = [(mine, 0, wide), (theirs, wide, wide)]
    if rem:
        spans += [
            (pl.multiple_of(core * feat + wide, 64), 2 * wide, rem),
            (pl.multiple_of(other * feat + wide, 64), 2 * wide + rem, rem),
        ]
    w1_copies = [
        pltpu.make_async_copy(w1_h.at[pl.ds(src, size)], w1.at[pl.ds(dst, size)], w1_sem.at[n])
        for n, (src, dst, size) in enumerate(spans)
    ]
    half_out = w2.shape[2]
    w2_copies = [
        pltpu.make_async_copy(
            w2_h.at[:, pl.ds(pl.multiple_of(side * half_out, LANES), half_out)], w2.at[n], w2_sem.at[n]
        )
        for n, side in enumerate((other, core))
    ]
    for copy in w1_copies + w2_copies:
        copy.start()

    lane = lax.broadcasted_iota(jnp.int32, route_src.shape, 1)
    route = jnp.full(route_src.shape, -1, jnp.int32)
    for s in range(samples):
        route = jnp.where(lane == s, seq_s[s] * samples + slot_s[s], route)
    route_src[...] = route
    routes[0] = route

    per = LANES // cap
    windows = lax.broadcasted_iota(jnp.int32, (BLOCK, LANES), 0)
    lanes_at = lax.broadcasted_iota(jnp.int32, (BLOCK, LANES), 1)

    def pool(s):
        pair, part = divmod(s, per)
        start = part * cap
        ids = jnp.concatenate([win_v[s : s + 1, :]] * per, axis=1)
        live = (lanes_at >= start) & (lanes_at < start + jnp.minimum(cnt_s[s], cap))
        hot = jnp.where((ids == windows) & live, 1.0, 0.0)
        number = jnp.sum(hot, axis=1, keepdims=True)
        total = lax.dot_general(
            hot.astype(jnp.bfloat16), enc[pair], (((1,), (1,)), ((), ())),
            preferred_element_type=jnp.float32,
        )
        y = (total * (1.0 / jnp.maximum(number, 1.0))).astype(jnp.bfloat16)
        for c in range(full):
            pooled[s, c * BLOCK : (c + 1) * BLOCK, :] = y[:, c * LANES : (c + 1) * LANES]
        if rem:
            tail = y[:, wide:]
            mid = BLOCK // 2
            pooled[s, full * BLOCK :, :] = jnp.concatenate([tail[:mid], tail[mid:]], axis=1)

    def pick(peer):
        chosen = jnp.int32(0)
        for s in range(1, samples):
            chosen = jnp.where(seq_s[s] == peer, jnp.int32(s), chosen)
        return pooled[chosen]

    half = groups // 2
    mine_base = me // half * half
    far_base = half - mine_base

    def far_first(i):
        far = lax.rem(me + i, half)
        near = lax.rem(me + i + 1, half)
        late = i // half
        peer = (1 - late) * (far_base + far) + late * (mine_base + near)
        return lax.rem(peer - me + groups, groups)

    def far_source(i):
        far = lax.rem(me - i + groups, half)
        near = lax.rem(me - i - 1 + 2 * groups, half)
        late = i // half
        peer = (1 - late) * (far_base + far) + late * (mine_base + near)
        return lax.rem(me - peer + groups, groups)

    def fill(j):
        outgo[j] = pick(lax.rem(me + j, groups))

    def data_copy(j):
        return pltpu.make_async_remote_copy(
            src_ref=outgo.at[j], dst_ref=arr.at[j], send_sem=send_sem.at[j], recv_sem=recv_sem.at[j],
            device_id={"dp": lax.rem(me + j, groups)}, device_id_type=MESH,
        )

    def route_copy(j):
        return pltpu.make_async_remote_copy(
            src_ref=route_src, dst_ref=routes.at[j], send_sem=rsend_sem.at[j], recv_sem=rrecv_sem.at[j],
            device_id={"dp": lax.rem(me + j, groups)}, device_id_type=MESH,
        )

    def forward(j):
        return pltpu.make_async_remote_copy(
            src_ref=arr.at[j], dst_ref=sib.at[j], send_sem=fsend_sem.at[j], recv_sem=frecv_sem.at[j],
            device_id={"tensor": other}, device_id_type=MESH,
        )

    for s in range(samples):
        if s % per == 0:
            enc_copies[s // per].wait()
        pool(s)
    loop(2, lambda i: fill(far_first(i)))
    pl.semaphore_wait(barrier, groups)
    loop(groups - 1, lambda i: route_copy(i + 1).start())

    def stage(i):
        fill(far_first(i + 2))
        data_copy(far_first(i)).start()

    loop(groups - 3, stage)
    arr[0] = pick(me)
    data_copy(far_first(groups - 3)).start()
    data_copy(far_first(groups - 2)).start()
    forward(0).start()

    loop(groups - 1, lambda i: route_copy(i + 1).wait_recv())

    table = routes[...]
    source = lax.broadcasted_iota(jnp.int32, table.shape, 0)
    picks = [
        jnp.minimum(jnp.sum(jnp.where(table == me * samples + k, source, 0)), groups - 1)
        for k in range(samples)
    ]
    def arrive(i):
        j = far_source(i)
        data_copy(j).wait_recv()
        forward(j).start()

    loop(groups - 1, arrive)
    loop(groups, lambda i: forward(i).wait_recv())

    for k in range(samples):
        rows = slice(k * BLOCK, (k + 1) * BLOCK)
        for c in range(full):
            lanes = slice(c * LANES, (c + 1) * LANES)
            xbuf[rows, lanes] = arr[picks[k], c * BLOCK : (c + 1) * BLOCK, :]
            lanes = slice(wide + c * LANES, wide + (c + 1) * LANES)
            xbuf[rows, lanes] = sib[picks[k], c * BLOCK : (c + 1) * BLOCK, :]
        if rem:
            a = arr[picks[k], full * BLOCK :, :]
            b = sib[picks[k], full * BLOCK :, :]
            mid = BLOCK // 2
            lo = k * BLOCK
            xbuf[lo : lo + mid, 2 * wide :] = jnp.concatenate([a[:, :rem], b[:, :rem]], axis=1)
            xbuf[lo + mid : lo + 2 * mid, 2 * wide :] = jnp.concatenate([a[:, rem:], b[:, rem:]], axis=1)

    for copy in w1_copies:
        copy.wait()
    total_rows = samples * BLOCK
    step = min(256, total_rows)

    def first_layer(m):
        rows = pl.ds(m * step, step) if isinstance(m, int) else pl.ds(pl.multiple_of(m * step, step), step)
        for lo, size in col_chunks(w1.shape[1], 768):
            acc = jnp.dot(xbuf[rows, :], w1[:, lo : lo + size], preferred_element_type=jnp.float32)
            hidden[rows, lo : lo + size] = gelu(acc + b1_v[lo : lo + size]).astype(jnp.bfloat16)

    tiles = total_rows // step
    if tiles == 1:
        first_layer(0)
    else:
        pl.loop(0, tiles)(first_layer)
    for copy in w2_copies:
        copy.wait()

    chunks = col_chunks(half_out, 384)

    def part_copy(n):
        lo, size = chunks[n]
        return pltpu.make_async_remote_copy(
            src_ref=part_out.at[:, lo : lo + size], dst_ref=part_in.at[:, lo : lo + size],
            send_sem=psend_sem.at[n], recv_sem=precv_sem.at[n],
            device_id={"tensor": other}, device_id_type=MESH,
        )

    def over_rows(body):
        if tiles == 1:
            body(slice(0, step))
        else:

            @pl.loop(0, tiles)
            def _(m):
                body(pl.ds(pl.multiple_of(m * step, step), step))

    for n, (lo, size) in enumerate(chunks):

        def send_part(rows):
            part_out[rows, lo : lo + size] = jnp.dot(
                hidden[rows, :], w2[0, :, lo : lo + size], preferred_element_type=jnp.float32
            ).astype(jnp.bfloat16)

        over_rows(send_part)
        if n:
            part_copy(n - 1).start()
    for n, (lo, size) in enumerate(chunks):

        def keep_part(rows):
            out_v[rows, lo : lo + size] = jnp.dot(
                hidden[rows, :], w2[1, :, lo : lo + size], preferred_element_type=jnp.float32
            ).astype(jnp.bfloat16)

        over_rows(keep_part)
        if n == 0:
            part_copy(len(chunks) - 1).start()
    for n, (lo, size) in enumerate(chunks):
        part_copy(n).wait_recv()

        def finish(rows):
            lanes = slice(lo, lo + size)
            both = out_v[rows, lanes].astype(jnp.float32) + part_in[rows, lanes].astype(jnp.float32)
            out_v[rows, lanes] = (both + b2_v[lanes]).astype(jnp.bfloat16)

        over_rows(finish)
    loop(groups, lambda i: forward(i).wait_send())

    def drain(i):
        data_copy(i + 1).wait_send()
        route_copy(i + 1).wait_send()

    loop(groups - 1, drain)
    for n in range(len(chunks)):
        part_copy(n).wait_send()


def shards(encoded, counts, win_ids, dest_seq, dest_slot, w_first, b_first, w_second, b_second):
    samples, cap = win_ids.shape
    feat = encoded.shape[1]
    groups = lax.axis_size("dp")
    hid = w_first.shape[1]
    half_out = b_second.shape[0]
    rows = samples * BLOCK
    block_rows = BLOCK * feat // LANES
    chunks = len(col_chunks(half_out, 384))
    vmem = pl.BlockSpec(memory_space=pltpu.VMEM)
    smem = pl.BlockSpec(memory_space=pltpu.SMEM)
    hbm = pl.BlockSpec(memory_space=pltpu.HBM)
    bf16 = jnp.bfloat16
    dma = pltpu.SemaphoreType.DMA
    return pl.pallas_call(
        functools.partial(kernel, (groups, samples, cap, feat)),
        out_shape=jax.ShapeDtypeStruct((rows, half_out), bf16),
        in_specs=[smem, smem, smem, vmem, vmem, vmem, hbm, hbm, hbm],
        out_specs=vmem,
        scratch_shapes=[
            pltpu.VMEM((samples * cap // LANES, feat, LANES), bf16),
            pltpu.VMEM((2 * feat, hid), bf16),
            pltpu.VMEM((2, hid, half_out), bf16),
            pltpu.VMEM((samples, block_rows, LANES), bf16),
            pltpu.VMEM((groups, block_rows, LANES), bf16),
            pltpu.VMEM((groups, block_rows, LANES), bf16),
            pltpu.VMEM((groups, block_rows, LANES), bf16),
            pltpu.VMEM((1, LANES), jnp.int32),
            pltpu.VMEM((groups, 1, LANES), jnp.int32),
            pltpu.VMEM((rows, 2 * feat), bf16),
            pltpu.VMEM((rows, hid), bf16),
            pltpu.VMEM((rows, half_out), bf16),
            pltpu.VMEM((rows, half_out), bf16),
            dma((samples * cap // LANES,)), dma((4,)), dma((2,)),
            dma((groups,)), dma((groups,)), dma((groups,)), dma((groups,)), dma((groups,)), dma((groups,)),
            dma((chunks,)), dma((chunks,)),
        ],
        compiler_params=pltpu.CompilerParams(
            collective_id=0, has_side_effects=True, vmem_limit_bytes=60 * 1024 * 1024
        ),
    )(
        dest_seq, dest_slot, counts, win_ids, b_first, b_second, encoded.T, w_first, w_second,
    )


def solution(mesh):
    placed = (
        P("dp", "tensor"), P("dp"), P("dp", None), P("dp"), P("dp"),
        P(None, "tensor"), P("tensor"), P("tensor", None), P("tensor"),
    )
    return jax.shard_map(
        shards, mesh=mesh, in_specs=placed, out_specs=P("dp", "tensor"), check_vma=False
    )
```

profile of v0, /device:TPU:0, one launch (start us, length us, event | category | flops | bytes accessed | tf_op | source)
XLA Modules:
  0.0 35.8 jit_solution(13958118269306976978)
XLA Ops:
  0.0 33.8 %shard_map.91 = bf16[256,1152]{1,0:T(8,128)(2,1)} custom-call(s32[8]{0:T(128)} %seq_s.1, s32[8]{0:T(128)} %slot_s.1, s32[8]{0:T(128)} %cnt_s.1, s32[8,64]{1,0:T(8,128)} %win_v.1, f32[2304]{0:T(1024)} %b1_v.1, f32[1152]{0:T(1024)} %b2_v.1, bf16[576,512]{1,0:T(8,128)(2,1)} %bitcast.1, bf16[1152,2304]{1,0:T(8,128)(2,1)} %w1_h.1, bf16[2304,2304]{1,0:T(8,128)(2,1)} %w2_h.1), custom_call_target="tpu_custom_call" | custom-call | tf_op jit(solution)/shard_map/pallas_call | solution.py:309
  33.8 1.9 %copy.11 = bf16[256,1152]{1,0:T(8,128)(2,1)} copy(bf16[256,1152]{1,0:T(8,128)(2,1)} %shard_map.91) | data formatting | bytes 1179648
where the time goes:
time: 36 us; the launch traced here: 35.8 us
  Pallas kernels  33.8 us (94%)
  local copies, waits for them, and re-layouts  1.92 us (5%)
    pallas_call x1, Pallas kernels, shards(): pl.pallas_call(functools.partial(kernel, (groups, samples, cap, feat)), o...  33.8 us
    unnamed x1, local copies, waits for them, and re-layouts  1.92 us

commit v1 on v0

--- a/solution.py
+++ b/solution.py
@@ -37,10 +37,10 @@
 
 def kernel(
     dims,
-    seq_s, slot_s, cnt_s, win_v, b1_v, b2_v, enc_h, w1_h, w2_h,
+    seq_h, slot_h, cnt_h, win_h, b1_h, b2_h, enc_h, w1_h, w2_h,
     out_v,
-    enc, w1, w2, pooled, outgo, arr, sib, route_src, routes, xbuf, hidden, part_out, part_in,
-    load_sem, w1_sem, w2_sem, send_sem, recv_sem, rsend_sem, rrecv_sem, fsend_sem, frecv_sem,
+    seq_s, slot_s, cnt_s, win_v, b1_v, b2_v, enc, w1, w2, pooled, outgo, arr, sib, route_src, routes, xbuf, hidden, part_out, part_in,
+    small_sem, load_sem, w1_sem, w2_sem, send_sem, recv_sem, rsend_sem, rrecv_sem, fsend_sem, frecv_sem,
     psend_sem, precv_sem,
 ):
     groups, samples, cap, feat = dims
@@ -65,6 +65,14 @@
         for p in range(pairs)
     ]
     for copy in enc_copies:
+        copy.start()
+    small = [
+        pltpu.make_async_copy(src, dst, small_sem.at[n])
+        for n, (src, dst) in enumerate(
+            [(seq_h, seq_s), (slot_h, slot_s), (cnt_h, cnt_s), (win_h, win_v), (b1_h, b1_v), (b2_h, b2_v)]
+        )
+    ]
+    for copy in small:
         copy.start()
 
     wide = full * LANES
@@ -87,6 +95,8 @@
         )
         for n, side in enumerate((other, core))
     ]
+    for copy in small[:4] + enc_copies:
+        copy.wait()
     for copy in w1_copies + w2_copies:
         copy.start()
 
@@ -166,8 +176,6 @@
         )
 
     for s in range(samples):
-        if s % per == 0:
-            enc_copies[s // per].wait()
         pool(s)
     loop(2, lambda i: fill(far_first(i)))
     pl.semaphore_wait(barrier, groups)
@@ -214,7 +222,7 @@
             xbuf[lo : lo + mid, 2 * wide :] = jnp.concatenate([a[:, :rem], b[:, :rem]], axis=1)
             xbuf[lo + mid : lo + 2 * mid, 2 * wide :] = jnp.concatenate([a[:, rem:], b[:, rem:]], axis=1)
 
-    for copy in w1_copies:
+    for copy in w1_copies + small[4:]:
         copy.wait()
     total_rows = samples * BLOCK
     step = min(256, total_rows)
@@ -302,16 +310,17 @@
     block_rows = BLOCK * feat // LANES
     chunks = len(col_chunks(half_out, 384))
     vmem = pl.BlockSpec(memory_space=pltpu.VMEM)
-    smem = pl.BlockSpec(memory_space=pltpu.SMEM)
     hbm = pl.BlockSpec(memory_space=pltpu.HBM)
     bf16 = jnp.bfloat16
     dma = pltpu.SemaphoreType.DMA
     return pl.pallas_call(
         functools.partial(kernel, (groups, samples, cap, feat)),
-        out_shape=jax.ShapeDtypeStruct((rows, half_out), bf16),
-        in_specs=[smem, smem, smem, vmem, vmem, vmem, hbm, hbm, hbm],
+        out_shape=pltpu.VMEM((rows, half_out), bf16),
+        in_specs=[hbm] * 9,
         out_specs=vmem,
         scratch_shapes=[
+            pltpu.SMEM((samples,), jnp.int32), pltpu.SMEM((samples,), jnp.int32), pltpu.SMEM((samples,), jnp.int32),
+            pltpu.VMEM((samples, cap), jnp.int32), pltpu.VMEM((hid,), jnp.float32), pltpu.VMEM((half_out,), jnp.float32),
             pltpu.VMEM((samples * cap // LANES, feat, LANES), bf16),
             pltpu.VMEM((2 * feat, hid), bf16),
             pltpu.VMEM((2, hid, half_out), bf16),
@@ -325,7 +334,7 @@
             pltpu.VMEM((rows, hid), bf16),
             pltpu.VMEM((rows, half_out), bf16),
             pltpu.VMEM((rows, half_out), bf16),
-            dma((samples * cap // LANES,)), dma((4,)), dma((2,)),
+            dma((6,)), dma((samples * cap // LANES,)), dma((4,)), dma((2,)),
             dma((groups,)), dma((groups,)), dma((groups,)), dma((groups,)), dma((groups,)), dma((groups,)),
             dma((chunks,)), dma((chunks,)),
         ],

time: 36 us -> 30.8 us (0.86)
  Pallas kernels: 33.8 us -> 29.7 us
  local copies, waits for them, and re-layouts: 1.92 us -> 0.82 us
    pallas_call x1, Pallas kernels: 33.8 us -> 29.7 us  [shards(): pl.pallas_call(functools.partial(kernel, (groups, samples, cap, feat)), o...]
    unnamed x1, local copies, waits for them, and re-layouts: 1.92 us -> 0.82 us
where the time goes in v1:
time: 30.8 us; the launch traced here: 30.5 us
  Pallas kernels  29.7 us (96%)
  local copies, waits for them, and re-layouts  0.82 us (3%)
    pallas_call x1, Pallas kernels, shards(): pl.pallas_call(functools.partial(kernel, (groups, samples, cap, feat)), o...  29.7 us
    unnamed x1, local copies, waits for them, and re-layouts  0.82 us

profile of v1, /device:TPU:0, one launch (start us, length us, event | category | flops | bytes accessed | tf_op | source)
XLA Modules:
  0.0 30.5 jit_solution(5223609088173935799)
XLA Ops:
  0.0 29.7 %shard_map.91 = bf16[256,1152]{1,0:T(8,128)(2,1)S(1)} custom-call(s32[8]{0:T(128)} %seq_h.1, s32[8]{0:T(128)} %slot_h.1, s32[8]{0:T(128)} %cnt_h.1, s32[8,64]{1,0:T(8,128)} %win_h.1, f32[2304]{0:T(1024)} %b1_h.1, f32[1152]{0:T(1024)} %b2_h.1, bf16[576,512]{1,0:T(8,128)(2,1)} %bitcast.1, bf16[1152,2304]{1,0:T(8,128)(2,1)} %w1_h.1, bf16[2304,2304]{1,0:T(8,128)(2,1)} %w2_h.1), custom_call_target="tpu_custom_call" | custom-call | tf_op jit(solution)/shard_map/pallas_call | solution.py:316
  29.7 0.8 %copy.11 = bf16[256,1152]{1,0:T(8,128)(2,1)} copy(bf16[256,1152]{1,0:T(8,128)(2,1)S(1)} %shard_map.91) | data formatting | bytes 1179648

commit v2 on v1

v2 whole, which is shorter than its diff:
```python
import functools
import math

import jax
import jax.numpy as jnp
from jax import lax
from jax.experimental import pallas as pl
from jax.experimental.pallas import tpu as pltpu
from jax.sharding import PartitionSpec as P

BLOCK = 32
LANES = 128
WIDE = 512
MESH = pl.DeviceIdType.MESH
UNROLL_MAX = 16
scope = jax.named_scope


def loop(count, body):
    if count <= UNROLL_MAX:
        for i in range(count):
            body(i)
    else:

        @pl.loop(0, count)
        def _(i):
            body(i)


def col_chunks(lo, hi, step):
    return [(at, min(step, hi - at)) for at in range(lo, hi, step)]


def gelu(x):
    c0 = math.sqrt(2.0 / math.pi)
    half = 0.5 * x
    return half + half * jnp.tanh(x * (c0 + (c0 * 0.044715) * (x * x)))


def exchange_masks(groups):
    quarter, half = groups // 4, groups // 2
    bits = quarter.bit_length() - 1
    plane = [int(format(g, f"0{bits}b")[::-1], 2) if bits else 0 for g in range(quarter)]
    near = [m for m in plane] + [quarter + m for m in plane]
    far = [half + z * quarter + m for m in plane for z in (1, 0)]
    return near + far


def flip(me, mask, groups):
    total, bit = 0, 1
    while bit < groups:
        own = lax.rem(me // bit, 2)
        total = total + bit * ((1 - own) if mask & bit else own)
        bit *= 2
    return total


def kernel(
    dims,
    seq_h, slot_h, cnt_h, win_h, b1_h, b2_h, enc_h, w1_h, w2_h,
    out_v,
    seq_s, slot_s, cnt_s, win_v, b1_v, b2_v, val_s, pick_s, rank_s,
    enc, w1, w2, pooled, outgo, arr_a, arr_b, sib_a, sib_b, route_src, routes,
    x_mine, x_sib, pre, hidden, keep, *rest,
):
    groups, samples, cap, feat, parts = dims
    part_out, part_in = rest[:parts], rest[parts : 2 * parts]
    (small_sem, load_sem, w1_sem, w2_sem, send_sem, recv_sem, rsend_sem, rrecv_sem, fsend_sem, frecv_sem,
     psend_sem, precv_sem) = rest[2 * parts :]
    full = feat // LANES
    rem = feat - full * LANES
    wide = full * LANES
    hid = w1.shape[2]
    half_out = b2_v.shape[0]
    first = arr_a.shape[0]
    ranks = samples // 2
    tile = ranks * BLOCK
    me = lax.axis_index("dp")
    core = lax.axis_index("tensor")
    other = 1 - core
    masks = exchange_masks(groups)
    peers = [flip(me, mask, groups) for mask in masks]
    order = list(range(1, groups))

    barrier = pltpu.get_barrier_semaphore()
    for o in range(1, groups):
        pl.semaphore_signal(barrier, 1, device_id={"dp": peers[o]}, device_id_type=MESH)
    pl.semaphore_signal(barrier, 1, device_id={"tensor": other}, device_id_type=MESH)

    pairs = enc.shape[0]
    enc_copies = [
        pltpu.make_async_copy(enc_h.at[:, p * LANES : (p + 1) * LANES], enc.at[p], load_sem.at[p])
        for p in range(pairs)
    ]
    small = [
        pltpu.make_async_copy(src, dst, small_sem.at[n])
        for n, (src, dst) in enumerate(
            [(seq_h, seq_s), (slot_h, slot_s), (cnt_h, cnt_s), (win_h, win_v), (b1_h, b1_v), (b2_h, b2_v)]
        )
    ]
    for copy in small[:4] + enc_copies + small[4:]:
        copy.start()
    w1_copies = [
        pltpu.make_async_copy(w1_h.at[pl.ds(pl.multiple_of(side * feat, 64), feat)], w1.at[n], w1_sem.at[n])
        for n, side in enumerate((core, other))
    ]
    w2_copies = [
        pltpu.make_async_copy(
            w2_h.at[:, pl.ds(pl.multiple_of(side * half_out, LANES), half_out)],
            w2.at[:, n * half_out : (n + 1) * half_out], w2_sem.at[n],
        )
        for n, side in enumerate((other, core))
    ]
    with scope("loadwait"):
        for copy in small[:4] + enc_copies:
            copy.wait()
    for copy in w1_copies + w2_copies:
        copy.start()

    lane = lax.broadcasted_iota(jnp.int32, route_src.shape, 1)
    route = jnp.full(route_src.shape, -1, jnp.int32)
    for s in range(samples):
        route = jnp.where(lane == s, seq_s[s] * samples + slot_s[s], route)
    route_src[...] = route
    routes[0] = route

    per = LANES // cap
    windows = lax.broadcasted_iota(jnp.int32, (BLOCK, LANES), 0)
    lanes_at = lax.broadcasted_iota(jnp.int32, (BLOCK, LANES), 1)

    def pool(s):
        pair, part = divmod(s, per)
        start = part * cap
        ids = jnp.concatenate([win_v[s : s + 1, :]] * per, axis=1)
        live = (lanes_at >= start) & (lanes_at < start + jnp.minimum(cnt_s[s], cap))
        hot = jnp.where((ids == windows) & live, 1.0, 0.0)
        number = jnp.sum(hot, axis=1, keepdims=True)
        total = lax.dot_general(
            hot.astype(jnp.bfloat16), enc[pair], (((1,), (1,)), ((), ())),
            preferred_element_type=jnp.float32,
        )
        y = (total * (1.0 / jnp.maximum(number, 1.0))).astype(jnp.bfloat16)
        for c in range(full):
            pooled[s, c * BLOCK : (c + 1) * BLOCK, :] = y[:, c * LANES : (c + 1) * LANES]
        if rem:
            tail = y[:, wide:]
            mid = BLOCK // 2
            pooled[s, full * BLOCK :, :] = jnp.concatenate([tail[:mid], tail[mid:]], axis=1)

    def pick(peer):
        chosen = jnp.int32(0)
        for s in range(1, samples):
            chosen = jnp.where(seq_s[s] == peer, jnp.int32(s), chosen)
        return pooled[chosen]

    def place(o, near_ref, late_ref):
        return near_ref.at[o] if o < first else late_ref.at[o - first]

    def data_copy(o):
        return pltpu.make_async_remote_copy(
            src_ref=outgo.at[o], dst_ref=place(o, arr_a, arr_b), send_sem=send_sem.at[o], recv_sem=recv_sem.at[o],
            device_id={"dp": peers[o]}, device_id_type=MESH,
        )

    def route_copy(o):
        return pltpu.make_async_remote_copy(
            src_ref=route_src, dst_ref=routes.at[o], send_sem=rsend_sem.at[o], recv_sem=rrecv_sem.at[o],
            device_id={"dp": peers[o]}, device_id_type=MESH,
        )

    def forward(o):
        return pltpu.make_async_remote_copy(
            src_ref=place(o, arr_a, arr_b), dst_ref=place(o, sib_a, sib_b),
            send_sem=fsend_sem.at[o], recv_sem=frecv_sem.at[o],
            device_id={"tensor": other}, device_id_type=MESH,
        )

    with scope("pool"):
        for s in range(samples):
            pool(s)

    def fill(o):
        outgo[o] = pick(peers[o])

    ahead = 2
    for o in order[:ahead]:
        fill(o)
    with scope("barrier"):
        pl.semaphore_wait(barrier, groups)
    with scope("stage"):
        for o in order:
            route_copy(o).start()
        for n, o in enumerate(order):
            if n + ahead < len(order):
                fill(order[n + ahead])
            else:
                arr_a[0] = pick(me)
            data_copy(o).start()
        forward(0).start()

    with scope("routewait"):
        for o in order:
            route_copy(o).wait_recv()
    base = me * samples
    seen = jnp.int32(0)
    for o in range(groups):
        row = routes[o]
        hit = (row >= base) & (row < base + samples)
        value = jnp.sum(jnp.where(hit, row - base + 1, 0))
        val_s[o] = value
        val_s[groups + o] = seen
        seen = seen + jnp.minimum(value, 1)

    def find(r):
        at, spot = jnp.int32(0), jnp.int32(0)
        for o in range(groups):
            value, before = val_s[o], val_s[groups + o]
            at = jnp.where((value > 0) & (before == r), o, at)
            spot = jnp.where(value == r + 1, before, spot)
        pick_s[r] = at
        rank_s[r] = jnp.minimum(spot, samples - 1)

    with scope("picks"):
        loop(samples, find)

    def arrive(o):
        with scope(f"arr{o}"):
            data_copy(o).wait_recv()
        forward(o).start()

    def unpack(dst, r, block):
        lo = r * BLOCK if isinstance(r, int) else pl.multiple_of(r * BLOCK, BLOCK)
        for c in range(full):
            dst[pl.ds(lo, BLOCK), c * LANES : (c + 1) * LANES] = block[c * BLOCK : (c + 1) * BLOCK]
        if rem:
            mid = BLOCK // 2
            tail = block[full * BLOCK :]
            dst[pl.ds(lo, mid), wide:] = tail[:, :rem]
            dst[pl.ds(lo + mid, mid), wide:] = tail[:, rem:]

    def early(dst, ref):
        def one(r):
            unpack(dst, r, ref[jnp.minimum(pick_s[r], first - 1)])

        loop(ranks, one)

    def late(dst, ref, ref_late):
        def one(r):
            at = pick_s[ranks + r]
            a = ref[jnp.minimum(at, first - 1)]
            b = ref_late[jnp.maximum(at - first, 0)]
            unpack(dst, r, jnp.where(at < first, a, b))

        loop(ranks, one)

    step = min(256, tile)

    def over_rows(body):
        if tile == step:
            body(slice(0, step), 0)
        else:

            @pl.loop(0, tile // step)
            def _(m):
                body(pl.ds(pl.multiple_of(m * step, step), step), m * (step // BLOCK))

    up_chunks = col_chunks(0, hid, 768)

    def mine_part(rows, _):
        for lo, size in up_chunks:
            pre[rows, lo : lo + size] = jnp.dot(
                x_mine[rows, :], w1[0, :, lo : lo + size], preferred_element_type=jnp.float32
            )

    def sib_part(rows, _):
        for lo, size in up_chunks:
            acc = jnp.dot(x_sib[rows, :], w1[1, :, lo : lo + size], preferred_element_type=jnp.float32)
            acc = acc + pre[rows, lo : lo + size] + b1_v[lo : lo + size]
            hidden[rows, lo : lo + size] = gelu(acc).astype(jnp.bfloat16)

    outs = col_chunks(0, half_out, WIDE)
    even = half_out // 256 * 256
    spans = col_chunks(0, even, WIDE)
    if even < half_out:
        spans = spans + [(even, 256)]
    spans = spans + col_chunks(sum(spans[-1]), 2 * half_out, WIDE)

    def down(which, lo, size):
        def body(rows, at):
            y = jnp.dot(
                hidden[rows, :], w2[:, lo : lo + size], preferred_element_type=jnp.float32
            ).astype(jnp.bfloat16)
            for n, (start, width) in enumerate(outs):
                begin, end = max(lo, start), min(lo + size, start + width)
                if begin < end:
                    for r in range(step // BLOCK):
                        part_out[n][which * ranks + at + r, :, begin - start : end - start] = y[
                            r * BLOCK : (r + 1) * BLOCK, begin - lo : end - lo
                        ]
            begin = max(lo, half_out)
            if begin < lo + size:
                for r in range(step // BLOCK):
                    keep[which * ranks + at + r, :, begin - half_out : lo + size - half_out] = y[
                        r * BLOCK : (r + 1) * BLOCK, begin - lo :
                    ]

        over_rows(body)

    def part_copy(which, n):
        span = pl.ds(which * ranks, ranks)
        return pltpu.make_async_remote_copy(
            src_ref=part_out[n].at[span], dst_ref=part_in[n].at[span],
            send_sem=psend_sem.at[which * parts + n], recv_sem=precv_sem.at[which * parts + n],
            device_id={"tensor": other}, device_id_type=MESH,
        )

    def project(which, between):
        sent = 0
        for at, (lo, size) in enumerate(spans):
            with scope(f"down{which}_{at}"):
                down(which, lo, size)
            while sent < parts and sum(outs[sent]) <= spans[at - 1][0] + spans[at - 1][1] and at:
                part_copy(which, sent).start()
                sent += 1
            between(at)

    for o in range(1, first):
        arrive(o)
    with scope("fwdA"):
        for o in range(first):
            forward(o).wait_recv()
    with scope("xA"):
        early(x_mine, arr_a)
        early(x_sib, sib_a)
    with scope("w1wait"):
        for copy in w1_copies + small[4:]:
            copy.wait()
    with scope("upA"):
        over_rows(mine_part)
        over_rows(sib_part)
    pending = list(range(first, groups))
    share = max(1, len(pending) // 4)

    def take(_):
        for o in pending[:share]:
            arrive(o)
        del pending[:share]

    take(0)
    with scope("w2wait"):
        for copy in w2_copies:
            copy.wait()
    project(0, lambda at: take(0) if at in (2, len(spans) - 1) else None)
    while pending:
        take(0)
    with scope("xBm"):
        late(x_mine, arr_a, arr_b)
    with scope("upBm"):
        over_rows(mine_part)
    with scope("fwdB"):
        for o in range(first, groups):
            forward(o).wait_recv()
    with scope("xBs"):
        late(x_sib, sib_a, sib_b)
    with scope("upBs"):
        over_rows(sib_part)
    project(1, lambda at: None)
    for n, (lo, size) in enumerate(outs):
        with scope(f"pwait{n}"):
            part_copy(0, n).wait_recv()
            part_copy(1, n).wait_recv()

        def finish(k):
            r = rank_s[k]
            rows = pl.ds(k * BLOCK if isinstance(k, int) else pl.multiple_of(k * BLOCK, BLOCK), BLOCK)
            both = keep[r, :, lo : lo + size].astype(jnp.float32) + part_in[n][r].astype(jnp.float32)
            out_v[rows, lo : lo + size] = (both + b2_v[lo : lo + size]).astype(jnp.bfloat16)

        with scope(f"finish{n}"):
            loop(samples, finish)
    with scope("drain"):
        for o in range(groups):
            forward(o).wait_send()
        for o in order:
            data_copy(o).wait_send()
            route_copy(o).wait_send()
        for which in range(2):
            for n in range(parts):
                part_copy(which, n).wait_send()


def shards(encoded, counts, win_ids, dest_seq, dest_slot, w_first, b_first, w_second, b_second):
    samples, cap = win_ids.shape
    feat = encoded.shape[1]
    groups = lax.axis_size("dp")
    hid = w_first.shape[1]
    half_out = b_second.shape[0]
    rows = samples * BLOCK
    tile = rows // 2
    block_rows = BLOCK * feat // LANES
    outs = col_chunks(0, half_out, WIDE)
    parts = len(outs)
    late = samples // 2
    first = groups - late
    hbm = pl.BlockSpec(memory_space=pltpu.HBM)
    bf16, f32, i32 = jnp.bfloat16, jnp.float32, jnp.int32
    vmem, smem, dma = pltpu.VMEM, pltpu.SMEM, pltpu.SemaphoreType.DMA
    return pl.pallas_call(
        functools.partial(kernel, (groups, samples, cap, feat, parts)),
        out_shape=vmem((rows, half_out), bf16),
        in_specs=[hbm] * 9,
        out_specs=pl.BlockSpec(memory_space=pltpu.VMEM),
        scratch_shapes=[
            smem((samples,), i32), smem((samples,), i32), smem((samples,), i32),
            vmem((samples, cap), i32), vmem((hid,), f32), vmem((half_out,), f32),
            smem((2 * groups,), i32), smem((samples,), i32), smem((samples,), i32),
            vmem((samples * cap // LANES, feat, LANES), bf16),
            vmem((2, feat, hid), bf16),
            vmem((hid, 2 * half_out), bf16),
            vmem((samples, block_rows, LANES), bf16),
            vmem((groups, block_rows, LANES), bf16),
            vmem((first, block_rows, LANES), bf16),
            vmem((late, block_rows, LANES), bf16),
            vmem((first, block_rows, LANES), bf16),
            vmem((late, block_rows, LANES), bf16),
            vmem((1, LANES), i32),
            vmem((groups, 1, LANES), i32),
            vmem((tile, feat), bf16),
            vmem((tile, feat), bf16),
            vmem((tile, hid), f32),
            vmem((tile, hid), bf16),
            vmem((samples, BLOCK, half_out), bf16),
            *[vmem((samples, BLOCK, size), bf16) for _, size in outs],
            *[vmem((samples, BLOCK, size), bf16) for _, size in outs],
            dma((6,)), dma((samples * cap // LANES,)), dma((2,)), dma((2,)),
            dma((groups,)), dma((groups,)), dma((groups,)), dma((groups,)), dma((groups,)), dma((groups,)),
            dma((2 * parts,)), dma((2 * parts,)),
        ],
        compiler_params=pltpu.CompilerParams(
            collective_id=0, has_side_effects=True, vmem_limit_bytes=60 * 1024 * 1024
        ),
    )(
        dest_seq, dest_slot, counts, win_ids, b_first, b_second, encoded.T, w_first, w_second,
    )


def solution(mesh):
    placed = (
        P("dp", "tensor"), P("dp"), P("dp", None), P("dp"), P("dp"),
        P(None, "tensor"), P("tensor"), P("tensor", None), P("tensor"),
    )
    return jax.shard_map(
        shards, mesh=mesh, in_specs=placed, out_specs=P("dp", "tensor"), check_vma=False
    )
```

time: 30.8 us -> 29.6 us (0.961)
  Pallas kernels: 29.7 us -> 28.7 us
    pallas_call x1, Pallas kernels: 29.7 us -> 28.7 us  [shards(): pl.pallas_call(functools.partial(kernel, (groups, samples, cap, feat, par...]
where the time goes in v2:
time: 29.6 us; the launch traced here: 29.5 us
  Pallas kernels  28.7 us (97%)
  local copies, waits for them, and re-layouts  0.82 us (3%)
    pallas_call x1, Pallas kernels, shards(): pl.pallas_call(functools.partial(kernel, (groups, samples, cap, feat, par...  28.7 us
    unnamed x1, local copies, waits for them, and re-layouts  0.82 us

profile of v2, /device:TPU:0, one launch (start us, length us, event | category | flops | bytes accessed | tf_op | source)
XLA Modules:
  0.0 29.5 jit_solution(14595615929014892422)
XLA Ops:
  0.0 28.7 %shard_map.91 = bf16[256,1152]{1,0:T(8,128)(2,1)S(1)} custom-call(s32[8]{0:T(128)} %seq_h.1, s32[8]{0:T(128)} %slot_h.1, s32[8]{0:T(128)} %cnt_h.1, s32[8,64]{1,0:T(8,128)} %win_h.1, f32[2304]{0:T(1024)} %b1_h.1, f32[1152]{0:T(1024)} %b2_h.1, bf16[576,512]{1,0:T(8,128)(2,1)} %bitcast.1, bf16[1152,2304]{1,0:T(8,128)(2,1)} %w1_h.1, bf16[2304,2304]{1,0:T(8,128)(2,1)} %w2_h.1), custom_call_target="tpu_custom_call" | custom-call | tf_op jit(solution)/shard_map/pallas_call | solution.py:408
  28.7 0.8 %copy.11 = bf16[256,1152]{1,0:T(8,128)(2,1)} copy(bf16[256,1152]{1,0:T(8,128)(2,1)S(1)} %shard_map.91) | data formatting | bytes 1179648

commit v3 on v2

--- a/solution.py
+++ b/solution.py
@@ -35,6 +35,10 @@
     c0 = math.sqrt(2.0 / math.pi)
     half = 0.5 * x
     return half + half * jnp.tanh(x * (c0 + (c0 * 0.044715) * (x * x)))
+
+
+def settle(ref, sem):
+    pltpu.make_async_copy(ref, ref, sem).wait()
 
 
 def exchange_masks(groups):
@@ -65,8 +69,7 @@
 ):
     groups, samples, cap, feat, parts = dims
     part_out, part_in = rest[:parts], rest[parts : 2 * parts]
-    (small_sem, load_sem, w1_sem, w2_sem, send_sem, recv_sem, rsend_sem, rrecv_sem, fsend_sem, frecv_sem,
-     psend_sem, precv_sem) = rest[2 * parts :]
+    small_sem, load_sem, send_sem, recv_sem, group_sem, psend_sem, precv_sem = rest[2 * parts :]
     full = feat // LANES
     rem = feat - full * LANES
     wide = full * LANES
@@ -81,6 +84,9 @@
     masks = exchange_masks(groups)
     peers = [flip(me, mask, groups) for mask in masks]
     order = list(range(1, groups))
+    half = groups // 2
+    depth = me // (groups // 4)
+    inner = lax.rem((depth + 1) // 2, 2)
 
     barrier = pltpu.get_barrier_semaphore()
     for o in range(1, groups):
@@ -89,7 +95,7 @@
 
     pairs = enc.shape[0]
     enc_copies = [
-        pltpu.make_async_copy(enc_h.at[:, p * LANES : (p + 1) * LANES], enc.at[p], load_sem.at[p])
+        pltpu.make_async_copy(enc_h.at[:, p * LANES : (p + 1) * LANES], enc.at[p], load_sem.at[0])
         for p in range(pairs)
     ]
     small = [
@@ -101,19 +107,20 @@
     for copy in small[:4] + enc_copies + small[4:]:
         copy.start()
     w1_copies = [
-        pltpu.make_async_copy(w1_h.at[pl.ds(pl.multiple_of(side * feat, 64), feat)], w1.at[n], w1_sem.at[n])
+        pltpu.make_async_copy(w1_h.at[pl.ds(pl.multiple_of(side * feat, 64), feat)], w1.at[n], load_sem.at[1])
         for n, side in enumerate((core, other))
     ]
     w2_copies = [
         pltpu.make_async_copy(
             w2_h.at[:, pl.ds(pl.multiple_of(side * half_out, LANES), half_out)],
-            w2.at[:, n * half_out : (n + 1) * half_out], w2_sem.at[n],
+            w2.at[:, n * half_out : (n + 1) * half_out], load_sem.at[2],
         )
         for n, side in enumerate((other, core))
     ]
     with scope("loadwait"):
-        for copy in small[:4] + enc_copies:
+        for copy in small[:4]:
             copy.wait()
+        settle(enc, load_sem.at[0])
     for copy in w1_copies + w2_copies:
         copy.start()
 
@@ -125,14 +132,19 @@
     routes[0] = route
 
     per = LANES // cap
-    windows = lax.broadcasted_iota(jnp.int32, (BLOCK, LANES), 0)
-    lanes_at = lax.broadcasted_iota(jnp.int32, (BLOCK, LANES), 1)
-
-    def pool(s):
-        pair, part = divmod(s, per)
-        start = part * cap
-        ids = jnp.concatenate([win_v[s : s + 1, :]] * per, axis=1)
-        live = (lanes_at >= start) & (lanes_at < start + jnp.minimum(cnt_s[s], cap))
+    tall = per * BLOCK
+    row_at = lax.broadcasted_iota(jnp.int32, (tall, LANES), 0)
+    lane_at = lax.broadcasted_iota(jnp.int32, (tall, LANES), 1)
+    windows = lax.rem(row_at, BLOCK)
+    slot_at = lane_at - row_at // BLOCK * cap
+
+    def pool(pair):
+        at = pair * per
+        ids = jnp.concatenate([win_v[at + n : at + n + 1, :] for n in range(per)], axis=1)
+        limit = jnp.full((tall, LANES), jnp.minimum(cnt_s[at], cap))
+        for n in range(1, per):
+            limit = jnp.where(row_at >= n * BLOCK, jnp.minimum(cnt_s[at + n], cap), limit)
+        live = (slot_at >= 0) & (slot_at < limit)
         hot = jnp.where((ids == windows) & live, 1.0, 0.0)
         number = jnp.sum(hot, axis=1, keepdims=True)
         total = lax.dot_general(
@@ -140,12 +152,14 @@
             preferred_element_type=jnp.float32,
         )
         y = (total * (1.0 / jnp.maximum(number, 1.0))).astype(jnp.bfloat16)
-        for c in range(full):
-            pooled[s, c * BLOCK : (c + 1) * BLOCK, :] = y[:, c * LANES : (c + 1) * LANES]
-        if rem:
-            tail = y[:, wide:]
-            mid = BLOCK // 2
-            pooled[s, full * BLOCK :, :] = jnp.concatenate([tail[:mid], tail[mid:]], axis=1)
+        for n in range(per):
+            rows = y[n * BLOCK : (n + 1) * BLOCK]
+            for c in range(full):
+                pooled[at + n, c * BLOCK : (c + 1) * BLOCK, :] = rows[:, c * LANES : (c + 1) * LANES]
+            if rem:
+                tail = rows[:, wide:]
+                mid = BLOCK // 2
+                pooled[at + n, full * BLOCK :, :] = jnp.concatenate([tail[:mid], tail[mid:]], axis=1)
 
     def pick(peer):
         chosen = jnp.int32(0)
@@ -156,31 +170,48 @@
     def place(o, near_ref, late_ref):
         return near_ref.at[o] if o < first else late_ref.at[o - first]
 
+    def swapped(o):
+        if o < half:
+            return o, peers[o]
+        low = o - (o - half) % 2
+        lead = inner if o == low else 1 - inner
+        return low + lead, lead * peers[low + 1] + (1 - lead) * peers[low]
+
+    def send(o):
+        slot, peer = swapped(o)
+        home, at = (arr_a, slot) if o < first else (arr_b, slot - first)
+        return pltpu.make_async_remote_copy(
+            src_ref=outgo.at[slot], dst_ref=home.at[at], send_sem=send_sem.at[0], recv_sem=recv_sem.at[slot],
+            device_id={"dp": peer}, device_id_type=MESH,
+        )
+
     def data_copy(o):
         return pltpu.make_async_remote_copy(
-            src_ref=outgo.at[o], dst_ref=place(o, arr_a, arr_b), send_sem=send_sem.at[o], recv_sem=recv_sem.at[o],
+            src_ref=outgo.at[o], dst_ref=place(o, arr_a, arr_b), send_sem=send_sem.at[0], recv_sem=recv_sem.at[o],
             device_id={"dp": peers[o]}, device_id_type=MESH,
         )
 
     def route_copy(o):
         return pltpu.make_async_remote_copy(
-            src_ref=route_src, dst_ref=routes.at[o], send_sem=rsend_sem.at[o], recv_sem=rrecv_sem.at[o],
+            src_ref=route_src, dst_ref=routes.at[o], send_sem=send_sem.at[1], recv_sem=group_sem.at[0],
             device_id={"dp": peers[o]}, device_id_type=MESH,
         )
 
     def forward(o):
+        late_slot = int(o >= first)
         return pltpu.make_async_remote_copy(
             src_ref=place(o, arr_a, arr_b), dst_ref=place(o, sib_a, sib_b),
-            send_sem=fsend_sem.at[o], recv_sem=frecv_sem.at[o],
+            send_sem=send_sem.at[2 + late_slot], recv_sem=group_sem.at[1 + late_slot],
             device_id={"tensor": other}, device_id_type=MESH,
         )
 
     with scope("pool"):
-        for s in range(samples):
-            pool(s)
+        for pair in range(pairs):
+            pool(pair)
 
     def fill(o):
-        outgo[o] = pick(peers[o])
+        slot, peer = swapped(o)
+        outgo[slot] = pick(peer)
 
     ahead = 2
     for o in order[:ahead]:
@@ -190,17 +221,22 @@
     with scope("stage"):
         for o in order:
             route_copy(o).start()
-        for n, o in enumerate(order):
-            if n + ahead < len(order):
-                fill(order[n + ahead])
-            else:
-                arr_a[0] = pick(me)
-            data_copy(o).start()
+        for n, o in enumerate(order[: first - 1]):
+            fill(order[n + ahead])
+            send(o).start()
+        for o in order[first - 1 + ahead :]:
+            fill(o)
+        arr_a[0] = pick(me)
+
+        @pl.when(core == 0)
+        def _():
+            for o in order[first - 1 :]:
+                send(o).start()
+
         forward(0).start()
 
     with scope("routewait"):
-        for o in order:
-            route_copy(o).wait_recv()
+        settle(routes.at[1:], group_sem.at[0])
     base = me * samples
     seen = jnp.int32(0)
     for o in range(groups):
@@ -310,65 +346,61 @@
         span = pl.ds(which * ranks, ranks)
         return pltpu.make_async_remote_copy(
             src_ref=part_out[n].at[span], dst_ref=part_in[n].at[span],
-            send_sem=psend_sem.at[which * parts + n], recv_sem=precv_sem.at[which * parts + n],
+            send_sem=psend_sem.at[n], recv_sem=precv_sem.at[n],
             device_id={"tensor": other}, device_id_type=MESH,
         )
 
-    def project(which, between):
-        sent = 0
-        for at, (lo, size) in enumerate(spans):
-            with scope(f"down{which}_{at}"):
-                down(which, lo, size)
-            while sent < parts and sum(outs[sent]) <= spans[at - 1][0] + spans[at - 1][1] and at:
-                part_copy(which, sent).start()
-                sent += 1
-            between(at)
+    def project(which):
+        with scope(f"send{which}"):
+            for lo, size in spans:
+                if lo < half_out:
+                    down(which, lo, size)
+        for n in range(parts):
+            part_copy(which, n).start()
+        with scope(f"keep{which}"):
+            for lo, size in spans:
+                if lo >= half_out:
+                    down(which, lo, size)
 
     for o in range(1, first):
         arrive(o)
+
+    @pl.when(core == 1)
+    def _():
+        for o in order[first - 1 :]:
+            send(o).start()
+
     with scope("fwdA"):
-        for o in range(first):
-            forward(o).wait_recv()
+        settle(sib_a, group_sem.at[1])
     with scope("xA"):
         early(x_mine, arr_a)
         early(x_sib, sib_a)
     with scope("w1wait"):
-        for copy in w1_copies + small[4:]:
+        settle(w1, load_sem.at[1])
+        for copy in small[4:]:
             copy.wait()
     with scope("upA"):
         over_rows(mine_part)
         over_rows(sib_part)
-    pending = list(range(first, groups))
-    share = max(1, len(pending) // 4)
-
-    def take(_):
-        for o in pending[:share]:
-            arrive(o)
-        del pending[:share]
-
-    take(0)
     with scope("w2wait"):
-        for copy in w2_copies:
-            copy.wait()
-    project(0, lambda at: take(0) if at in (2, len(spans) - 1) else None)
-    while pending:
-        take(0)
+        settle(w2, load_sem.at[2])
+    project(0)
+    for o in range(first, groups):
+        arrive(o)
     with scope("xBm"):
         late(x_mine, arr_a, arr_b)
     with scope("upBm"):
         over_rows(mine_part)
     with scope("fwdB"):
-        for o in range(first, groups):
-            forward(o).wait_recv()
+        settle(sib_b, group_sem.at[2])
     with scope("xBs"):
         late(x_sib, sib_a, sib_b)
     with scope("upBs"):
         over_rows(sib_part)
-    project(1, lambda at: None)
+    project(1)
     for n, (lo, size) in enumerate(outs):
         with scope(f"pwait{n}"):
-            part_copy(0, n).wait_recv()
-            part_copy(1, n).wait_recv()
+            settle(part_in[n], precv_sem.at[n])
 
         def finish(k):
             r = rank_s[k]
@@ -379,14 +411,12 @@
         with scope(f"finish{n}"):
             loop(samples, finish)
     with scope("drain"):
-        for o in range(groups):
-            forward(o).wait_send()
-        for o in order:
-            data_copy(o).wait_send()
-            route_copy(o).wait_send()
-        for which in range(2):
-            for n in range(parts):
-                part_copy(which, n).wait_send()
+        settle(arr_a, send_sem.at[2])
+        settle(arr_b, send_sem.at[3])
+        settle(outgo.at[1:], send_sem.at[0])
+        settle(routes.at[1:], send_sem.at[1])
+        for n in range(parts):
+            settle(part_out[n], psend_sem.at[n])
 
 
 def shards(encoded, counts, win_ids, dest_seq, dest_slot, w_first, b_first, w_second, b_second):
@@ -432,9 +462,7 @@
             vmem((samples, BLOCK, half_out), bf16),
             *[vmem((samples, BLOCK, size), bf16) for _, size in outs],
             *[vmem((samples, BLOCK, size), bf16) for _, size in outs],
-            dma((6,)), dma((samples * cap // LANES,)), dma((2,)), dma((2,)),
-            dma((groups,)), dma((groups,)), dma((groups,)), dma((groups,)), dma((groups,)), dma((groups,)),
-            dma((2 * parts,)), dma((2 * parts,)),
+            dma((6,)), dma((3,)), dma((4,)), dma((groups,)), dma((3,)), dma((parts,)), dma((parts,)),
         ],
         compiler_params=pltpu.CompilerParams(
             collective_id=0, has_side_effects=True, vmem_limit_bytes=60 * 1024 * 1024

time: 29.6 us -> 25.5 us (0.86)
  Pallas kernels: 28.7 us -> 24.5 us
    pallas_call x1, Pallas kernels: 28.7 us -> 24.5 us  [shards(): pl.pallas_call(functools.partial(kernel, (groups, samples, cap, feat, par...]
where the time goes in v3:
time: 25.5 us; the launch traced here: 25.4 us
  Pallas kernels  24.5 us (96%)
  local copies, waits for them, and re-layouts  0.82 us (3%)
    pallas_call x1, Pallas kernels, shards(): pl.pallas_call(functools.partial(kernel, (groups, samples, cap, feat, par...  24.5 us
    unnamed x1, local copies, waits for them, and re-layouts  0.82 us

profile of v3, /device:TPU:0, one launch (start us, length us, event | category | flops | bytes accessed | tf_op | source)
XLA Modules:
  0.0 25.4 jit_solution(18199079099152784677)
XLA Ops:
  0.0 24.5 %shard_map.91 = bf16[256,1152]{1,0:T(8,128)(2,1)S(1)} custom-call(s32[8]{0:T(128)} %seq_h.1, s32[8]{0:T(128)} %slot_h.1, s32[8]{0:T(128)} %cnt_h.1, s32[8,64]{1,0:T(8,128)} %win_h.1, f32[2304]{0:T(1024)} %b1_h.1, f32[1152]{0:T(1024)} %b2_h.1, bf16[576,512]{1,0:T(8,128)(2,1)} %bitcast.1, bf16[1152,2304]{1,0:T(8,128)(2,1)} %w1_h.1, bf16[2304,2304]{1,0:T(8,128)(2,1)} %w2_h.1), custom_call_target="tpu_custom_call" | custom-call | tf_op jit(solution)/shard_map/pallas_call | solution.py:438
  24.5 0.8 %copy.11 = bf16[256,1152]{1,0:T(8,128)(2,1)} copy(bf16[256,1152]{1,0:T(8,128)(2,1)S(1)} %shard_map.91) | data formatting | bytes 1179648

commit v4 on v3

--- a/solution.py
+++ b/solution.py
@@ -83,8 +83,10 @@
     other = 1 - core
     masks = exchange_masks(groups)
     peers = [flip(me, mask, groups) for mask in masks]
-    order = list(range(1, groups))
     half = groups // 2
+    order = [*range(half // 2, half), *range(1, half // 2)]
+    for lo, hi in ((half, first), (first, groups)):
+        order += [*range(lo, hi, 2), *range(lo + 1, hi, 2)]
     depth = me // (groups // 4)
     inner = lax.rem((depth + 1) // 2, 2)
 
@@ -93,10 +95,10 @@
         pl.semaphore_signal(barrier, 1, device_id={"dp": peers[o]}, device_id_type=MESH)
     pl.semaphore_signal(barrier, 1, device_id={"tensor": other}, device_id_type=MESH)
 
-    pairs = enc.shape[0]
+    pairs = samples * cap // LANES
     enc_copies = [
-        pltpu.make_async_copy(enc_h.at[:, p * LANES : (p + 1) * LANES], enc.at[p], load_sem.at[0])
-        for p in range(pairs)
+        pltpu.make_async_copy(enc_h.at[lo : lo + size], enc.at[lo : lo + size], load_sem.at[0])
+        for lo, size in col_chunks(0, feat, 144)
     ]
     small = [
         pltpu.make_async_copy(src, dst, small_sem.at[n])
@@ -148,7 +150,7 @@
         hot = jnp.where((ids == windows) & live, 1.0, 0.0)
         number = jnp.sum(hot, axis=1, keepdims=True)
         total = lax.dot_general(
-            hot.astype(jnp.bfloat16), enc[pair], (((1,), (1,)), ((), ())),
+            hot.astype(jnp.bfloat16), enc[:, pair * LANES : (pair + 1) * LANES], (((1,), (1,)), ((), ())),
             preferred_element_type=jnp.float32,
         )
         y = (total * (1.0 / jnp.maximum(number, 1.0))).astype(jnp.bfloat16)
@@ -362,13 +364,16 @@
                 if lo >= half_out:
                     down(which, lo, size)
 
-    for o in range(1, first):
+    for o in range(1, 8):
         arrive(o)
 
     @pl.when(core == 1)
     def _():
         for o in order[first - 1 :]:
             send(o).start()
+
+    for o in range(8, first):
+        arrive(o)
 
     with scope("fwdA"):
         settle(sib_a, group_sem.at[1])
@@ -444,7 +449,7 @@
             smem((samples,), i32), smem((samples,), i32), smem((samples,), i32),
             vmem((samples, cap), i32), vmem((hid,), f32), vmem((half_out,), f32),
             smem((2 * groups,), i32), smem((samples,), i32), smem((samples,), i32),
-            vmem((samples * cap // LANES, feat, LANES), bf16),
+            vmem((feat, samples * cap), bf16),
             vmem((2, feat, hid), bf16),
             vmem((hid, 2 * half_out), bf16),
             vmem((samples, block_rows, LANES), bf16),

time: 25.5 us -> 25.1 us (0.984)
  Pallas kernels: 24.5 us -> 24.2 us
    pallas_call x1, Pallas kernels: 24.5 us -> 24.2 us  [shards(): pl.pallas_call(functools.partial(kernel, (groups, samples, cap, feat, par...]
where the time goes in v4:
time: 25.1 us; the launch traced here: 25 us
  Pallas kernels  24.2 us (96%)
  local copies, waits for them, and re-layouts  0.82 us (3%)
    pallas_call x1, Pallas kernels, shards(): pl.pallas_call(functools.partial(kernel, (groups, samples, cap, feat, par...  24.2 us
    unnamed x1, local copies, waits for them, and re-layouts  0.82 us

profile of v4, /device:TPU:0, one launch (start us, length us, event | category | flops | bytes accessed | tf_op | source)
XLA Modules:
  0.0 25.0 jit_solution(10803537242516864474)
XLA Ops:
  0.0 24.2 %shard_map.91 = bf16[256,1152]{1,0:T(8,128)(2,1)S(1)} custom-call(s32[8]{0:T(128)} %seq_h.1, s32[8]{0:T(128)} %slot_h.1, s32[8]{0:T(128)} %cnt_h.1, s32[8,64]{1,0:T(8,128)} %win_h.1, f32[2304]{0:T(1024)} %b1_h.1, f32[1152]{0:T(1024)} %b2_h.1, bf16[576,512]{1,0:T(8,128)(2,1)} %bitcast.1, bf16[1152,2304]{1,0:T(8,128)(2,1)} %w1_h.1, bf16[2304,2304]{1,0:T(8,128)(2,1)} %w2_h.1), custom_call_target="tpu_custom_call" | custom-call | tf_op jit(solution)/shard_map/pallas_call | solution.py:443
  24.2 0.8 %copy.11 = bf16[256,1152]{1,0:T(8,128)(2,1)} copy(bf16[256,1152]{1,0:T(8,128)(2,1)S(1)} %shard_map.91) | data formatting | bytes 1179648

commit v5 on v4

--- a/solution.py
+++ b/solution.py
@@ -69,7 +69,7 @@
 ):
     groups, samples, cap, feat, parts = dims
     part_out, part_in = rest[:parts], rest[parts : 2 * parts]
-    small_sem, load_sem, send_sem, recv_sem, group_sem, psend_sem, precv_sem = rest[2 * parts :]
+    ready_sem, small_sem, load_sem, send_sem, recv_sem, group_sem, psend_sem, precv_sem = rest[2 * parts :]
     full = feat // LANES
     rem = feat - full * LANES
     wide = full * LANES
@@ -84,16 +84,35 @@
     masks = exchange_masks(groups)
     peers = [flip(me, mask, groups) for mask in masks]
     half = groups // 2
-    order = [*range(half // 2, half), *range(1, half // 2)]
-    for lo, hi in ((half, first), (first, groups)):
-        order += [*range(lo, hi, 2), *range(lo + 1, hi, 2)]
+    near = [*range(half // 2, half), *range(1, half // 2)]
+    far_a = [*range(half, first, 2), *range(half + 1, first, 2)]
+    far_b = [*range(first, groups, 2), *range(first + 1, groups, 2)]
+    side = me // half
+    above = [lax.rem(me // (1 << max(mask.bit_length() - 1, 0)), 2) == 0 for mask in masks]
     depth = me // (groups // 4)
     inner = lax.rem((depth + 1) // 2, 2)
 
     barrier = pltpu.get_barrier_semaphore()
-    for o in range(1, groups):
+    pl.semaphore_signal(barrier, 1, device_id={"tensor": other}, device_id_type=MESH)
+    for o in range(1, half):
+
+        @pl.when(above[o] | (side == 0))
+        def _():
+            pl.semaphore_signal(barrier, 1, device_id={"dp": peers[o]}, device_id_type=MESH)
+
+    for o in range(half, groups):
         pl.semaphore_signal(barrier, 1, device_id={"dp": peers[o]}, device_id_type=MESH)
-    pl.semaphore_signal(barrier, 1, device_id={"tensor": other}, device_id_type=MESH)
+
+    def meet():
+        pl.semaphore_wait(barrier, side * (me + 1) + (1 - side) * groups)
+
+        @pl.when(side == 1)
+        def _():
+            for o in range(1, half):
+
+                @pl.when(jnp.logical_not(above[o]))
+                def _():
+                    pl.semaphore_signal(ready_sem.at[0], 1, device_id={"dp": peers[o]}, device_id_type=MESH)
 
     pairs = samples * cap // LANES
     enc_copies = [
@@ -119,6 +138,11 @@
         )
         for n, side in enumerate((other, core))
     ]
+
+    @pl.when(depth == 3)
+    def _():
+        meet()
+
     with scope("loadwait"):
         for copy in small[:4]:
             copy.wait()
@@ -215,51 +239,64 @@
         slot, peer = swapped(o)
         outgo[slot] = pick(peer)
 
-    ahead = 2
-    for o in order[:ahead]:
+    def launch(slots):
+        for o in slots:
+            send(o).start()
+
+    for o in far_a:
         fill(o)
     with scope("barrier"):
-        pl.semaphore_wait(barrier, groups)
+
+        @pl.when(depth != 3)
+        def _():
+            meet()
+
     with scope("stage"):
-        for o in order:
+
+        for o in range(half, groups):
             route_copy(o).start()
-        for n, o in enumerate(order[: first - 1]):
-            fill(order[n + ahead])
-            send(o).start()
-        for o in order[first - 1 + ahead :]:
+
+        @pl.when(side == 1)
+        def _():
+            launch(far_a)
+
+        for o in near:
+
+            @pl.when(jnp.logical_not(above[o]) | (side == 0))
+            def _():
+                route_copy(o).start()
+
+        for o in far_b + near:
             fill(o)
+
         arr_a[0] = pick(me)
-
-        @pl.when(core == 0)
+        for o in near:
+
+            @pl.when(jnp.logical_not(above[o]) | (side == 0))
+            def _():
+                send(o).start()
+
+        forward(0).start()
+    with scope("nearready"):
+
+        @pl.when((side == 1) & (me < groups - 1))
         def _():
-            for o in order[first - 1 :]:
-                send(o).start()
-
-        forward(0).start()
-
-    with scope("routewait"):
-        settle(routes.at[1:], group_sem.at[0])
-    base = me * samples
-    seen = jnp.int32(0)
-    for o in range(groups):
-        row = routes[o]
-        hit = (row >= base) & (row < base + samples)
-        value = jnp.sum(jnp.where(hit, row - base + 1, 0))
-        val_s[o] = value
-        val_s[groups + o] = seen
-        seen = seen + jnp.minimum(value, 1)
-
-    def find(r):
-        at, spot = jnp.int32(0), jnp.int32(0)
-        for o in range(groups):
-            value, before = val_s[o], val_s[groups + o]
-            at = jnp.where((value > 0) & (before == r), o, at)
-            spot = jnp.where(value == r + 1, before, spot)
-        pick_s[r] = at
-        rank_s[r] = jnp.minimum(spot, samples - 1)
-
-    with scope("picks"):
-        loop(samples, find)
+            pl.semaphore_wait(ready_sem.at[0], groups - 1 - me)
+
+    for slots, copy in ((near, route_copy), (near, send)):
+        for o in slots:
+
+            @pl.when(above[o] & (side == 1))
+            def _():
+                copy(o).start()
+
+    @pl.when(side == 0)
+    def _():
+        launch(far_a)
+
+    @pl.when(core == 0)
+    def _():
+        launch(far_b)
 
     def arrive(o):
         with scope(f"arr{o}"):
@@ -364,17 +401,39 @@
                 if lo >= half_out:
                     down(which, lo, size)
 
-    for o in range(1, 8):
+    for o in range(1, half):
         arrive(o)
 
     @pl.when(core == 1)
     def _():
-        for o in order[first - 1 :]:
-            send(o).start()
-
-    for o in range(8, first):
+        launch(far_b)
+
+    for o in range(half, first):
         arrive(o)
 
+    with scope("routewait"):
+        settle(routes.at[1:], group_sem.at[0])
+    base = me * samples
+    seen = jnp.int32(0)
+    for o in range(groups):
+        row = routes[o]
+        hit = (row >= base) & (row < base + samples)
+        value = jnp.sum(jnp.where(hit, row - base + 1, 0))
+        val_s[o] = value
+        val_s[groups + o] = seen
+        seen = seen + jnp.minimum(value, 1)
+
+    def find(r):
+        at, spot = jnp.int32(0), jnp.int32(0)
+        for o in range(groups):
+            value, before = val_s[o], val_s[groups + o]
+            at = jnp.where((value > 0) & (before == r), o, at)
+            spot = jnp.where(value == r + 1, before, spot)
+        pick_s[r] = at
+        rank_s[r] = jnp.minimum(spot, samples - 1)
+
+    with scope("picks"):
+        loop(samples, find)
     with scope("fwdA"):
         settle(sib_a, group_sem.at[1])
     with scope("xA"):
@@ -467,7 +526,7 @@
             vmem((samples, BLOCK, half_out), bf16),
             *[vmem((samples, BLOCK, size), bf16) for _, size in outs],
             *[vmem((samples, BLOCK, size), bf16) for _, size in outs],
-            dma((6,)), dma((3,)), dma((4,)), dma((groups,)), dma((3,)), dma((parts,)), dma((parts,)),
+            pltpu.SemaphoreType.REGULAR((1,)), dma((6,)), dma((3,)), dma((4,)), dma((groups,)), dma((3,)), dma((parts,)), dma((parts,)),
         ],
         compiler_params=pltpu.CompilerParams(
             collective_id=0, has_side_effects=True, vmem_limit_bytes=60 * 1024 * 1024

time: 25.1 us -> 24.6 us (0.980)
  Pallas kernels: 24.2 us -> 23.7 us
    pallas_call x1, Pallas kernels: 24.2 us -> 23.7 us  [shards(): pl.pallas_call(functools.partial(kernel, (groups, samples, cap, feat, par...]
where the time goes in v5:
time: 24.6 us; the launch traced here: 24.5 us
  Pallas kernels  23.7 us (96%)
  local copies, waits for them, and re-layouts  0.82 us (3%)
    pallas_call x1, Pallas kernels, shards(): pl.pallas_call(functools.partial(kernel, (groups, samples, cap, feat, par...  23.7 us
    unnamed x1, local copies, waits for them, and re-layouts  0.82 us

profile of v5, /device:TPU:0, one launch (start us, length us, event | category | flops | bytes accessed | tf_op | source)
XLA Modules:
  0.0 24.5 jit_solution(8689516229791273406)
XLA Ops:
  0.0 23.7 %shard_map.91 = bf16[256,1152]{1,0:T(8,128)(2,1)S(1)} custom-call(s32[8]{0:T(128)} %seq_h.1, s32[8]{0:T(128)} %slot_h.1, s32[8]{0:T(128)} %cnt_h.1, s32[8,64]{1,0:T(8,128)} %win_h.1, f32[2304]{0:T(1024)} %b1_h.1, f32[1152]{0:T(1024)} %b2_h.1, bf16[576,512]{1,0:T(8,128)(2,1)} %bitcast.1, bf16[1152,2304]{1,0:T(8,128)(2,1)} %w1_h.1, bf16[2304,2304]{1,0:T(8,128)(2,1)} %w2_h.1), custom_call_target="tpu_custom_call" | custom-call | tf_op jit(solution)/shard_map/pallas_call | solution.py:502
  23.7 0.8 %copy.11 = bf16[256,1152]{1,0:T(8,128)(2,1)} copy(bf16[256,1152]{1,0:T(8,128)(2,1)S(1)} %shard_map.91) | data formatting | bytes 1179648

commit v6 on v5

--- a/solution.py
+++ b/solution.py
@@ -193,9 +193,6 @@
             chosen = jnp.where(seq_s[s] == peer, jnp.int32(s), chosen)
         return pooled[chosen]
 
-    def place(o, near_ref, late_ref):
-        return near_ref.at[o] if o < first else late_ref.at[o - first]
-
     def swapped(o):
         if o < half:
             return o, peers[o]
@@ -207,14 +204,8 @@
         slot, peer = swapped(o)
         home, at = (arr_a, slot) if o < first else (arr_b, slot - first)
         return pltpu.make_async_remote_copy(
-            src_ref=outgo.at[slot], dst_ref=home.at[at], send_sem=send_sem.at[0], recv_sem=recv_sem.at[slot],
+            src_ref=outgo.at[slot], dst_ref=home.at[at], send_sem=send_sem.at[0], recv_sem=recv_sem.at[slot // 2],
             device_id={"dp": peer}, device_id_type=MESH,
-        )
-
-    def data_copy(o):
-        return pltpu.make_async_remote_copy(
-            src_ref=outgo.at[o], dst_ref=place(o, arr_a, arr_b), send_sem=send_sem.at[0], recv_sem=recv_sem.at[o],
-            device_id={"dp": peers[o]}, device_id_type=MESH,
         )
 
     def route_copy(o):
@@ -223,10 +214,13 @@
             device_id={"dp": peers[o]}, device_id_type=MESH,
         )
 
-    def forward(o):
-        late_slot = int(o >= first)
+    def span(lo, size, near_ref, late_ref):
+        return near_ref.at[pl.ds(lo, size)] if lo < first else late_ref.at[pl.ds(lo - first, size)]
+
+    def forward(lo, size):
+        late_slot = int(lo >= first)
         return pltpu.make_async_remote_copy(
-            src_ref=place(o, arr_a, arr_b), dst_ref=place(o, sib_a, sib_b),
+            src_ref=span(lo, size, arr_a, arr_b), dst_ref=span(lo, size, sib_a, sib_b),
             send_sem=send_sem.at[2 + late_slot], recv_sem=group_sem.at[1 + late_slot],
             device_id={"tensor": other}, device_id_type=MESH,
         )
@@ -276,7 +270,7 @@
             def _():
                 send(o).start()
 
-        forward(0).start()
+        forward(0, 1).start()
     with scope("nearready"):
 
         @pl.when((side == 1) & (me < groups - 1))
@@ -298,10 +292,12 @@
     def _():
         launch(far_b)
 
-    def arrive(o):
-        with scope(f"arr{o}"):
-            data_copy(o).wait_recv()
-        forward(o).start()
+    def arrive(lo, hi):
+        for at in range(lo, hi, 2):
+            start, size = (at, 2) if at else (1, 1)
+            with scope(f"arr{at}"):
+                settle(span(start, size, arr_a, arr_b), recv_sem.at[at // 2])
+            forward(start, size).start()
 
     def unpack(dst, r, block):
         lo = r * BLOCK if isinstance(r, int) else pl.multiple_of(r * BLOCK, BLOCK)
@@ -401,15 +397,13 @@
                 if lo >= half_out:
                     down(which, lo, size)
 
-    for o in range(1, half):
-        arrive(o)
+    arrive(0, half)
 
     @pl.when(core == 1)
     def _():
         launch(far_b)
 
-    for o in range(half, first):
-        arrive(o)
+    arrive(half, first)
 
     with scope("routewait"):
         settle(routes.at[1:], group_sem.at[0])
@@ -449,8 +443,7 @@
     with scope("w2wait"):
         settle(w2, load_sem.at[2])
     project(0)
-    for o in range(first, groups):
-        arrive(o)
+    arrive(first, groups)
     with scope("xBm"):
         late(x_mine, arr_a, arr_b)
     with scope("upBm"):
@@ -526,7 +519,7 @@
             vmem((samples, BLOCK, half_out), bf16),
             *[vmem((samples, BLOCK, size), bf16) for _, size in outs],
             *[vmem((samples, BLOCK, size), bf16) for _, size in outs],
-            pltpu.SemaphoreType.REGULAR((1,)), dma((6,)), dma((3,)), dma((4,)), dma((groups,)), dma((3,)), dma((parts,)), dma((parts,)),
+            pltpu.SemaphoreType.REGULAR((1,)), dma((6,)), dma((3,)), dma((4,)), dma((groups // 2,)), dma((3,)), dma((parts,)), dma((parts,)),
         ],
         compiler_params=pltpu.CompilerParams(
             collective_id=0, has_side_effects=True, vmem_limit_bytes=60 * 1024 * 1024

time: 24.6 us -> 24.6 us (level)
  no operation moved by 1% of the time
where the time goes in v6:
time: 24.6 us; the launch traced here: 24.4 us
  Pallas kernels  23.6 us (96%)
  local copies, waits for them, and re-layouts  0.82 us (3%)
    pallas_call x1, Pallas kernels, shards(): pl.pallas_call(functools.partial(kernel, (groups, samples, cap, feat, par...  23.6 us
    unnamed x1, local copies, waits for them, and re-layouts  0.82 us

profile of v6, /device:TPU:0, one launch (start us, length us, event | category | flops | bytes accessed | tf_op | source)
XLA Modules:
  0.0 24.4 jit_solution(8065349952296350345)
XLA Ops:
  0.0 23.6 %shard_map.91 = bf16[256,1152]{1,0:T(8,128)(2,1)S(1)} custom-call(s32[8]{0:T(128)} %seq_h.1, s32[8]{0:T(128)} %slot_h.1, s32[8]{0:T(128)} %cnt_h.1, s32[8,64]{1,0:T(8,128)} %win_h.1, f32[2304]{0:T(1024)} %b1_h.1, f32[1152]{0:T(1024)} %b2_h.1, bf16[576,512]{1,0:T(8,128)(2,1)} %bitcast.1, bf16[1152,2304]{1,0:T(8,128)(2,1)} %w1_h.1, bf16[2304,2304]{1,0:T(8,128)(2,1)} %w2_h.1), custom_call_target="tpu_custom_call" | custom-call | tf_op jit(solution)/shard_map/pallas_call | solution.py:495
  23.6 0.8 %copy.11 = bf16[256,1152]{1,0:T(8,128)(2,1)} copy(bf16[256,1152]{1,0:T(8,128)(2,1)S(1)} %shard_map.91) | data formatting | bytes 1179648
